TPU v7x, 32 devices: a whole 2x2x4 slice. The times are simulated.
32 devices in a mesh: region: 4 (over z), depth: 2 (over y), member: 4 (over x, core).
Axes of the slice: x: 2, y: 2, z: 4, core: 2. Of those that a mesh axis runs over, the one named last changes fastest.
Arguments:
- ensemble: bfloat16 [14, 384, 4096], P('depth', 'member', 'region'), may hold values from -6 to 6
- obs_weights: float32 [14], P('depth'), may hold values from -1.5 to 1.5
- obs_tiles: int32 [2048], P('region'), may hold values from 0 to 1023
- obs_values: float32 [2048], P('region'), may hold values from -8 to 8
- obs_error: float32 [2048], P('region'), may hold values from 0.2 to 2
- obs_noise: float32 [384, 2048], P('member', 'region'), may hold values from -6 to 6
Outputs:
- analysis: bfloat16 [14, 384, 4096], P('depth', 'member', 'region')
- inflation: float32 [], replicated
Inputs may be any that keep to these rules, and one draw needn't show every extreme that they name: `obs_tiles`: the tile of the observation, counted within the 1024 tiles of the region whose block holds the observation.
All inputs are finite; a program needn't handle non-finite values.
Results may differ from a plain program's by a relative error of at most 0.011.
Values may be sent and summed in bfloat16 or wider, within the bound.
A program may use at most 64 MiB of HBM per device.

v0:
```python
import jax
import jax.numpy as jnp
from jax import lax
from jax.sharding import PartitionSpec as P

MEMBERS = 384
RADIUS = 1024


def extended(array, sides, width):
    for axis, dim in sides:
        peers, length = (lax.axis_size(axis), array.shape[dim])
        up = [(i, (i + 1) % peers) for i in range(peers - 1)]
        down = [(j, i) for i, j in up]
        last = lax.slice_in_dim(array, length - width, length, axis=dim)
        leading = lax.slice_in_dim(array, 0, width, axis=dim)
        before = lax.ppermute(last, axis, up)
        after = lax.ppermute(leading, axis, down)
        array = jnp.concatenate([before, array, after], axis=dim)
    return array


def regress(
    anomalies, own_anom, state_mean, obs_anom, perturbed, factor, obs_pos, first_tile, infl_root
):
    var_count = anomalies.shape[0]
    tile_count = anomalies.shape[2]
    block = 128

    def one_block(block_index, output):
        block_start = block_index * block
        slab = lax.dynamic_slice_in_dim(anomalies, block_start, block, 2)
        own_slab = lax.dynamic_slice_in_dim(own_anom, block_start, block, 2)
        means = lax.dynamic_slice_in_dim(state_mean, block_start, block, 1)
        covariance = jnp.einsum(
            "lmt,mj->ltj", slab, obs_anom, preferred_element_type=jnp.float32
        ) / (MEMBERS - 1)
        tile_pos = (first_tile + block_start + jnp.arange(block, dtype=jnp.int32)).astype(
            jnp.float32
        )
        closeness = jnp.maximum(0.0, 1.0 - jnp.abs(tile_pos[:, None] - obs_pos[None, :]) / RADIUS)
        kalman_gain = (covariance * (closeness * closeness * factor[None, :])[None]).astype(
            jnp.bfloat16
        )
        increment = jnp.einsum(
            "ltj,mj->lmt", kalman_gain, perturbed, preferred_element_type=jnp.float32
        )
        updated = (means[:, None, :] + infl_root * own_slab.astype(jnp.float32) + increment).astype(
            jnp.bfloat16
        )
        return lax.dynamic_update_slice_in_dim(output, updated, block_start, 2)

    output = jnp.zeros((var_count, perturbed.shape[0], tile_count), jnp.bfloat16)
    return lax.fori_loop(0, tile_count // block, one_block, output)


def shards(ensemble, obs_weights, obs_tiles, obs_values, obs_error, obs_noise):
    tile_count = ensemble.shape[2]
    own_members = ensemble.shape[1]
    obs_count = obs_tiles.shape[0]
    member_sum = jnp.sum(ensemble, axis=1, dtype=jnp.float32)
    picked = jnp.take(ensemble, obs_tiles, axis=2).astype(jnp.float32)
    partial_pred = jnp.einsum("lmk,l->mk", picked, obs_weights, precision=lax.Precision.HIGHEST)
    predicted = lax.psum(partial_pred, "depth")
    totals = lax.psum(
        (member_sum, jnp.sum(predicted, axis=0), jnp.sum(predicted * predicted, axis=0)), "member"
    )
    state_mean = totals[0] / MEMBERS
    obs_mean = totals[1] / MEMBERS
    obs_dev = predicted - obs_mean[None, :]
    obs_spread = (totals[2] - MEMBERS * obs_mean * obs_mean) / (MEMBERS - 1)
    innovation = obs_values - obs_mean
    global_sums = lax.psum(
        (jnp.sum(innovation * innovation), jnp.sum(obs_spread + obs_error)), "region"
    )
    inflation = global_sums[0] / global_sums[1]
    infl_root = jnp.sqrt(inflation)
    factor = inflation / (inflation * obs_spread + obs_error)
    obs_anom = obs_dev.astype(jnp.bfloat16)
    perturbed = (
        innovation[None, :] + jnp.sqrt(obs_error)[None, :] * obs_noise - infl_root * obs_dev
    ).astype(jnp.bfloat16)
    first_tile = lax.axis_index("region") * tile_count
    obs_pos = (first_tile + obs_tiles).astype(jnp.float32)
    stacked = jnp.concatenate([obs_anom, perturbed], axis=0)
    widened = extended(stacked, (("region", 1),), obs_count)
    near_anom = widened[:own_members]
    near_pert = widened[own_members:]
    scalars = jnp.stack([factor, obs_pos], axis=0)
    wide_scalars = extended(scalars, (("region", 1),), obs_count)
    near_factor = wide_scalars[0]
    near_pos = wide_scalars[1]
    anomalies = (ensemble.astype(jnp.float32) - state_mean[:, None, :]).astype(jnp.bfloat16)
    all_anom, all_obs_anom = (
        lax.all_gather(anomalies, "member", axis=1, tiled=True),
        lax.all_gather(near_anom, "member", axis=0, tiled=True),
    )
    analysis = regress(
        all_anom,
        anomalies,
        state_mean,
        all_obs_anom,
        near_pert,
        near_factor,
        near_pos,
        first_tile,
        infl_root,
    )
    return (analysis, inflation)


def solution(mesh):
    return jax.shard_map(
        shards,
        mesh=mesh,
        in_specs=(
            P("depth", "member", "region"),
            P("depth"),
            P("region"),
            P("region"),
            P("region"),
            P("member", "region"),
        ),
        out_specs=(P("depth", "member", "region"), P()),
        check_vma=False,
    )
```

profile of v0, /device:TPU:0, one launch (start us, length us, event | category | flops | bytes accessed | tf_op | source)
XLA Modules:
  0.0 185.1 jit_solution(7628334277064460269)
XLA Ops:
  8.6 3.2 %copy.8 = bf16[7,96,1024]{1,0,2:T(8,128)(2,1)S(1)} copy(bf16[7,96,1024]{2,1,0:T(8,128)(2,1)} %param.8) | data formatting | bytes 2752512 | tf_op args[0]
  11.8 1.8 gather_fusion
  13.7 1.8 select_bitcast_fusion
  18.4 25.0 %all-reduce.4.cloned.1.call-done = f32[96,512]{1,0:T(8,128)} async-done(((f32[96,512]{1,0:T(8,128)}), f32[96,512]{1,0:T(8,128)}) %all-reduce.4.cloned.1.call-update) | async-done | bytes 196624 | tf_op jit(solution)/shard_map/psum | solution.py:64
  44.3 10.8 %all-reduce = (f32[7,1024]{1,0:T(8,128)S(1)}, f32[512]{0:T(512)S(1)}, f32[512]{0:T(512)S(1)}) all-reduce(f32[7,1024]{1,0:T(8,128)S(1)} %convert_reduce_fusion, f32[512]{0:T(512)S(1)} %get-tuple-element.188, f32[512]{0:T(512)S(1)} %get-tuple-element.187), channel_id=1, replica_groups=mesh['region'=4,'depth'=2,'member'=4] {'member'}, use_global_device_ids=true, to_apply=%region_1.2 | all-reduce | flops 8192 | bytes 65536 | tf_op jit(solution)/shard_map/psum | solution.py:65
  55.7 12.3 %all-reduce.1 = (f32[]{:T(128)}, f32[]{:T(128)}) all-reduce(f32[]{:T(128)} %get-tuple-element.216, f32[]{:T(128)} %get-tuple-element.229), channel_id=1, replica_groups=mesh['region'=4,'depth'=2,'member'=4] {'region'}, use_global_device_ids=true, to_apply=%region_6.7 | all-reduce | flops 2 | bytes 16 | tf_op jit(solution)/shard_map/psum | solution.py:73
  70.5 1.3 collective-permute-start.1
  71.8 4.6 %collective-permute-start = (bf16[192,512]{1,0:T(8,128)(2,1)S(1)}, bf16[192,512]{1,0:T(8,128)(2,1)S(1)}, u32[]{:S(2)}, u32[]{:S(2)}) collective-permute-start(bf16[192,512]{1,0:T(8,128)(2,1)S(1)} %pad_maximum_fusion.1), channel_id=1, source_target_pairs={{0,8},{8,16},{16,24},{1,9},{9,17},{17,25},{2,10},{10,18},{18,26},{... | collective-permute-start | bytes 589832 | tf_op jit(solution)/shard_map/ppermute | solution.py:17
  76.4 1.7 collective-permute-done.1
  78.1 1.5 collective-permute-done
  80.4 1.4 fusion.18
  83.2 5.0 %collective-permute-start.2 = (f32[2,512]{1,0:T(2,128)S(1)}, f32[2,512]{1,0:T(2,128)S(1)}, u32[]{:S(2)}, u32[]{:S(2)}) collective-permute-start(f32[2,512]{1,0:T(2,128)S(1)} %pad_maximum_fusion.3), channel_id=1, source_target_pairs={{0,8},{8,16},{16,24},{1,9},{9,17},{17,25},{2,10},{10,18},{18,26},{... | collective-permute-start | bytes 12296 | tf_op jit(solution)/shard_map/ppermute | solution.py:17
  88.2 1.3 collective-permute-done.2
  89.6 7.4 %all-gather.5.cloned.1.call-done = bf16[384,1536]{1,0:T(8,128)(2,1)} async-done(((bf16[96,1536]{1,0:T(8,128)(2,1)}), bf16[384,1536]{1,0:T(8,128)(2,1)}) %all-gather.5.cloned.1.call-update) | async-done | bytes 1179664 | tf_op jit(solution)/shard_map/all_gather | solution.py:96
  97.0 44.1 %all-gather.3.cloned.1.call-done = bf16[7,384,1024]{2,1,0:T(8,128)(2,1)} async-done(((bf16[7,96,1024]{2,1,0:T(8,128)(2,1)}), bf16[7,384,1024]{2,1,0:T(8,128)(2,1)}) %all-gather.3.cloned.1.call-update) | async-done | bytes 5505040 | tf_op jit(solution)/shard_map/all_gather | solution.py:95
  141.2 35.1 %while.13 = (s32[]{:T(128)}, bf16[7,96,1024]{2,1,0:T(8,128)(2,1)S(1)}, f32[7,1024]{1,0:T(8,128)S(1)}, f32[]{:T(128)}, bf16[7,96,1024]{2,1,0:T(8,128)(2,1)}, /*in...) while((s32[]{:T(128)}, ...), condition=%wide.region_12.13_spmd, body=%wide.region_11.12_spmd.sunk | while | flops 1325961472 | bytes 4130527 | solution.py:54
  141.6 4.0 %fusion.33 = bf16[7,96,1024]{2,1,0:T(8,128)(2,1)S(1)} fusion(bf16[7,96,1024]{2,1,0:T(8,128)(2,1)S(1)} %get-tuple-element.314, s32[]{:T(128)S(6)} %select_n.27, f32[128,1536]{1,0:T(8,128)S(1)} %multiply_multiply_fusion.2, bf16[384,1536]{1,0:T(8,128)(2,1)} %get-tuple-element.335, bf16[7,384,1024]{2,1,0:T(8,128)(2,1)} %get-tuple-element.334, ...), kind=kOutput, calls=%fused_computation.7.clone.1 | convolution fusion | flops 1324388352 | bytes 3298816 | tf_op jit(solution)/shard_map/while/body/eval_jaxpr/ltj,mj->lmt/dot_general | solution.py:45
  146.0 4.0 %fusion.33 = bf16[7,96,1024]{2,1,0:T(8,128)(2,1)S(1)} fusion(bf16[7,96,1024]{2,1,0:T(8,128)(2,1)S(1)} %get-tuple-element.314, s32[]{:T(128)S(6)} %select_n.27, f32[128,1536]{1,0:T(8,128)S(1)} %multiply_multiply_fusion.2, bf16[384,1536]{1,0:T(8,128)(2,1)} %get-tuple-element.335, bf16[7,384,1024]{2,1,0:T(8,128)(2,1)} %get-tuple-element.334, ...), kind=kOutput, calls=%fused_computation.7.clone.1 | convolution fusion | flops 1324388352 | bytes 3298816 | tf_op jit(solution)/shard_map/while/body/eval_jaxpr/ltj,mj->lmt/dot_general | solution.py:45
  150.4 4.0 %fusion.33 = bf16[7,96,1024]{2,1,0:T(8,128)(2,1)S(1)} fusion(bf16[7,96,1024]{2,1,0:T(8,128)(2,1)S(1)} %get-tuple-element.314, s32[]{:T(128)S(6)} %select_n.27, f32[128,1536]{1,0:T(8,128)S(1)} %multiply_multiply_fusion.2, bf16[384,1536]{1,0:T(8,128)(2,1)} %get-tuple-element.335, bf16[7,384,1024]{2,1,0:T(8,128)(2,1)} %get-tuple-element.334, ...), kind=kOutput, calls=%fused_computation.7.clone.1 | convolution fusion | flops 1324388352 | bytes 3298816 | tf_op jit(solution)/shard_map/while/body/eval_jaxpr/ltj,mj->lmt/dot_general | solution.py:45
  154.8 4.0 %fusion.33 = bf16[7,96,1024]{2,1,0:T(8,128)(2,1)S(1)} fusion(bf16[7,96,1024]{2,1,0:T(8,128)(2,1)S(1)} %get-tuple-element.314, s32[]{:T(128)S(6)} %select_n.27, f32[128,1536]{1,0:T(8,128)S(1)} %multiply_multiply_fusion.2, bf16[384,1536]{1,0:T(8,128)(2,1)} %get-tuple-element.335, bf16[7,384,1024]{2,1,0:T(8,128)(2,1)} %get-tuple-element.334, ...), kind=kOutput, calls=%fused_computation.7.clone.1 | convolution fusion | flops 1324388352 | bytes 3298816 | tf_op jit(solution)/shard_map/while/body/eval_jaxpr/ltj,mj->lmt/dot_general | solution.py:45
  159.2 4.0 %fusion.33 = bf16[7,96,1024]{2,1,0:T(8,128)(2,1)S(1)} fusion(bf16[7,96,1024]{2,1,0:T(8,128)(2,1)S(1)} %get-tuple-element.314, s32[]{:T(128)S(6)} %select_n.27, f32[128,1536]{1,0:T(8,128)S(1)} %multiply_multiply_fusion.2, bf16[384,1536]{1,0:T(8,128)(2,1)} %get-tuple-element.335, bf16[7,384,1024]{2,1,0:T(8,128)(2,1)} %get-tuple-element.334, ...), kind=kOutput, calls=%fused_computation.7.clone.1 | convolution fusion | flops 1324388352 | bytes 3298816 | tf_op jit(solution)/shard_map/while/body/eval_jaxpr/ltj,mj->lmt/dot_general | solution.py:45
  163.6 4.0 %fusion.33 = bf16[7,96,1024]{2,1,0:T(8,128)(2,1)S(1)} fusion(bf16[7,96,1024]{2,1,0:T(8,128)(2,1)S(1)} %get-tuple-element.314, s32[]{:T(128)S(6)} %select_n.27, f32[128,1536]{1,0:T(8,128)S(1)} %multiply_multiply_fusion.2, bf16[384,1536]{1,0:T(8,128)(2,1)} %get-tuple-element.335, bf16[7,384,1024]{2,1,0:T(8,128)(2,1)} %get-tuple-element.334, ...), kind=kOutput, calls=%fused_computation.7.clone.1 | convolution fusion | flops 1324388352 | bytes 3298816 | tf_op jit(solution)/shard_map/while/body/eval_jaxpr/ltj,mj->lmt/dot_general | solution.py:45
  167.9 4.0 %fusion.33 = bf16[7,96,1024]{2,1,0:T(8,128)(2,1)S(1)} fusion(bf16[7,96,1024]{2,1,0:T(8,128)(2,1)S(1)} %get-tuple-element.314, s32[]{:T(128)S(6)} %select_n.27, f32[128,1536]{1,0:T(8,128)S(1)} %multiply_multiply_fusion.2, bf16[384,1536]{1,0:T(8,128)(2,1)} %get-tuple-element.335, bf16[7,384,1024]{2,1,0:T(8,128)(2,1)} %get-tuple-element.334, ...), kind=kOutput, calls=%fused_computation.7.clone.1 | convolution fusion | flops 1324388352 | bytes 3298816 | tf_op jit(solution)/shard_map/while/body/eval_jaxpr/ltj,mj->lmt/dot_general | solution.py:45
  172.3 4.0 %fusion.33 = bf16[7,96,1024]{2,1,0:T(8,128)(2,1)S(1)} fusion(bf16[7,96,1024]{2,1,0:T(8,128)(2,1)S(1)} %get-tuple-element.314, s32[]{:T(128)S(6)} %select_n.27, f32[128,1536]{1,0:T(8,128)S(1)} %multiply_multiply_fusion.2, bf16[384,1536]{1,0:T(8,128)(2,1)} %get-tuple-element.335, bf16[7,384,1024]{2,1,0:T(8,128)(2,1)} %get-tuple-element.334, ...), kind=kOutput, calls=%fused_computation.7.clone.1 | convolution fusion | flops 1324388352 | bytes 3298816 | tf_op jit(solution)/shard_map/while/body/eval_jaxpr/ltj,mj->lmt/dot_general | solution.py:45
  (79 shorter events, 13.0 us)
Async XLA Ops:
  7.2 9.3 %copy-start = (f32[7]{0:T(128)S(1)}, f32[7]{0:T(128)}, u32[]{:S(2)}) copy-start(f32[7]{0:T(128)} %param.9) | copy-start | bytes 88
  7.2 36.1 %all-reduce.4.cloned.1.call-start = ((), (), s32[]{:S(2)}) async-start(), calls=%async_computation | async-start | bytes 393216 | tf_op jit(solution)/shard_map/psum | solution.py:64
  15.4 2.6 %copy-start.1 = (bf16[7,96,1024]{2,1,0:T(8,128)(2,1)S(1)}, bf16[7,96,1024]{2,1,0:T(8,128)(2,1)}, u32[]{:S(2)}) copy-start(bf16[7,96,1024]{2,1,0:T(8,128)(2,1)} %param.8) | copy-start | bytes 4128772
  16.5 38.6 %copy-start.4 = (f32[512]{0:T(512)S(1)}, f32[512]{0:T(512)}, u32[]{:S(2)}) copy-start(f32[512]{0:T(512)} %param.12) | copy-start | bytes 6148
  16.5 38.6 %copy-start.5 = (f32[512]{0:T(512)S(1)}, f32[512]{0:T(512)}, u32[]{:S(2)}) copy-start(f32[512]{0:T(512)} %param.11) | copy-start | bytes 6148
  17.3 52.2 %copy-start.3 = (f32[96,512]{1,0:T(8,128)S(1)}, f32[96,512]{1,0:T(8,128)}, u32[]{:S(2)}) copy-start(f32[96,512]{1,0:T(8,128)} %param.13) | copy-start | bytes 589828
  18.0 79.0 %all-gather.5.cloned.1.call-start = ((), (), s32[]{:S(2)}) async-start(), calls=%async_computation.2 | async-start | bytes 1474560 | tf_op jit(solution)/shard_map/all_gather | solution.py:96
  70.5 7.6 %collective-permute-start.1 = (bf16[192,512]{1,0:T(8,128)(2,1)S(1)}, bf16[192,512]{1,0:T(8,128)(2,1)S(1)}, u32[]{:S(2)}, u32[]{:S(2)}) collective-permute-start(bf16[192,512]{1,0:T(8,128)(2,1)S(1)} %pad_maximum_fusion.1), channel_id=1, source_target_pairs={{8,0},{16,8},{24,16},{9,1},{17,9},{25,17},{10,2},{18,10},{26,18},{... | collective-permute-start | bytes 589832 | tf_op jit(solution)/shard_map/ppermute | solution.py:18
  71.8 7.7 %collective-permute-start = (bf16[192,512]{1,0:T(8,128)(2,1)S(1)}, bf16[192,512]{1,0:T(8,128)(2,1)S(1)}, u32[]{:S(2)}, u32[]{:S(2)}) collective-permute-start(bf16[192,512]{1,0:T(8,128)(2,1)S(1)} %pad_maximum_fusion.1), channel_id=1, source_target_pairs={{0,8},{8,16},{16,24},{1,9},{9,17},{17,25},{2,10},{10,18},{18,26},{... | collective-permute-start | bytes 589832 | tf_op jit(solution)/shard_map/ppermute | solution.py:17
  80.4 60.7 %all-gather.3.cloned.1.call-start = ((), (), s32[]{:S(2)}) async-start(), calls=%async_computation.1 | async-start | bytes 6881280 | tf_op jit(solution)/shard_map/all_gather | solution.py:95
  81.9 6.3 %collective-permute-start.3 = (f32[2,512]{1,0:T(2,128)S(1)}, f32[2,512]{1,0:T(2,128)S(1)}, u32[]{:S(2)}, u32[]{:S(2)}) collective-permute-start(f32[2,512]{1,0:T(2,128)S(1)} %pad_maximum_fusion.3), channel_id=1, source_target_pairs={{8,0},{16,8},{24,16},{9,1},{17,9},{25,17},{10,2},{18,10},{26,18},{... | collective-permute-start | bytes 12296 | tf_op jit(solution)/shard_map/ppermute | solution.py:18
  83.2 6.3 %collective-permute-start.2 = (f32[2,512]{1,0:T(2,128)S(1)}, f32[2,512]{1,0:T(2,128)S(1)}, u32[]{:S(2)}, u32[]{:S(2)}) collective-permute-start(f32[2,512]{1,0:T(2,128)S(1)} %pad_maximum_fusion.3), channel_id=1, source_target_pairs={{0,8},{8,16},{16,24},{1,9},{9,17},{17,25},{2,10},{10,18},{18,26},{... | collective-permute-start | bytes 12296 | tf_op jit(solution)/shard_map/ppermute | solution.py:17
  176.3 1.1 copy-start.2
Sparse Core Ops, SparseCore 0:
  18.1 25.1 all-reduce.3
  80.5 16.4 all-gather.4
  99.1 41.8 all-gather.2
where the time goes:
time: 186 us; the launch traced here: 185 us
  waiting for transfers between devices  80.9 us (43%)
  matrix products  32.7 us (18%)
  blocking collectives  23.2 us (12%)
  between operations  16.5 us (9%)
  starting transfers between devices  12.3 us (7%)
  other arithmetic  10.1 us (5%)
  local copies, waits for them, and re-layouts  8.89 us (5%)
    all_gather x1, waiting for transfers between devices, shards(): lax.all_gather(anomalies, 'member', axis=1, tiled=True)  44.1 us
    dot_general x8, matrix products, one_block(): jnp.einsum('ltj,mj->lmt', kalman_gain, perturbed, preferred_element_type=...  31.9 us
    psum x1, waiting for transfers between devices, shards(): predicted = lax.psum(partial_pred, 'depth')  25 us
    psum x1, blocking collectives, shards(): lax.psum((jnp.sum(innovation * innovation), jnp.sum(obs_spread + obs_erro...  12.3 us
    psum x1, blocking collectives, shards(): lax.psum((member_sum, jnp.sum(predicted, axis=0), jnp.sum(predicted * pre...  10.8 us
    ppermute x2, starting transfers between devices, extended(): before = lax.ppermute(last, axis, up)  9.57 us
    all_gather x1, waiting for transfers between devices, shards(): lax.all_gather(near_anom, 'member', axis=0, tiled=True)  7.4 us
    unnamed x13, local copies, waits for them, and re-layouts  4.34 us
  transfers between devices with their start and end apart: 7, of which 6 were waited for; matrix products, arithmetic and copies ran while one was open for 1% of the time, Pallas kernels for 0%

commit v1 on v0

--- a/solution.py
+++ b/solution.py
@@ -61,7 +61,8 @@
     member_sum = jnp.sum(ensemble, axis=1, dtype=jnp.float32)
     picked = jnp.take(ensemble, obs_tiles, axis=2).astype(jnp.float32)
     partial_pred = jnp.einsum("lmk,l->mk", picked, obs_weights, precision=lax.Precision.HIGHEST)
-    predicted = lax.psum(partial_pred, "depth")
+    piece_out = jax.lax.all_gather(partial_pred, "depth")
+    predicted = jnp.sum(piece_out, axis=0)
     totals = lax.psum(
         (member_sum, jnp.sum(predicted, axis=0), jnp.sum(predicted * predicted, axis=0)), "member"
     )

time: 186 us -> 169 us (0.909)
  waiting for transfers between devices: 80.9 us -> 57.3 us
  blocking collectives: 23.2 us -> 31.8 us
    psum x1 -> x0, waiting for transfers between devices: 25 us -> none  [shards(): predicted = lax.psum(partial_pred, 'depth')]
    all_gather x0 -> x1, blocking collectives: none -> 8.56 us  [shards(): piece_out = jax.lax.all_gather(partial_pred, 'depth')]
    unnamed x13 -> x15, local copies, waits for them, and re-layouts: 4.34 us -> 3.25 us
  transfers between devices with their start and end apart: 7 -> 6, of which waited for: 6 -> 5; matrix products, arithmetic and copies ran while one was open for 1% -> 1% of each run, Pallas kernels for 0% -> 0%
where the time goes in v1:
time: 169 us
  waiting for transfers between devices  57.3 us (34%)
  matrix products  32.6 us (19%)
  blocking collectives  31.8 us (19%)
  between operations  16.8 us (10%)
  starting transfers between devices  12.2 us (7%)
  other arithmetic  9.73 us (6%)
  local copies, waits for them, and re-layouts  7.7 us (5%)
    all_gather x1, waiting for transfers between devices, shards(): lax.all_gather(anomalies, 'member', axis=1, tiled=True)  44.1 us
    dot_general x8, matrix products, one_block(): jnp.einsum('ltj,mj->lmt', kalman_gain, perturbed, preferred_element_type=...  31.8 us
    psum x1, blocking collectives, shards(): lax.psum((jnp.sum(innovation * innovation), jnp.sum(obs_spread + obs_erro...  12.6 us
    psum x1, blocking collectives, shards(): lax.psum((member_sum, jnp.sum(predicted, axis=0), jnp.sum(predicted * pre...  10.7 us
    ppermute x2, starting transfers between devices, extended(): before = lax.ppermute(last, axis, up)  9.57 us
    all_gather x1, waiting for transfers between devices, shards(): lax.all_gather(near_anom, 'member', axis=0, tiled=True)  8.7 us
    all_gather x1, blocking collectives, shards(): piece_out = jax.lax.all_gather(partial_pred, 'depth')  8.56 us
  transfers between devices with their start and end apart: 6, of which 5 were waited for; matrix products, arithmetic and copies ran while one was open for 1% of the time, Pallas kernels for 0%

profile of v1, /device:TPU:0, one launch (start us, length us, event | category | flops | bytes accessed | tf_op | source)
XLA Modules:
  0.0 168.7 jit_solution(17583082966844297893)
XLA Ops:
  7.2 1.7 %convert_reduce_fusion = f32[7,1024]{1,0:T(8,128)S(1)} fusion(bf16[7,96,1024]{2,1,0:T(8,128)(2,1)} %param.8), kind=kLoop, calls=%fused_computation.15 | loop fusion | flops 1369088 | bytes 1404928 | tf_op jit(solution)/shard_map/reduce_sum | solution.py:61
  9.0 2.1 %copy.11 = bf16[7,96,1024]{1,0,2:T(8,128)(2,1)S(1)} copy(bf16[7,96,1024]{2,1,0:T(8,128)(2,1)S(1)} %copy-done.1) | data formatting | bytes 2752512 | tf_op args[0]
  11.2 2.4 %gather_fusion = bf16[512,7,96]{2,1,0:T(8,128)(2,1)} fusion(bf16[7,96,1024]{1,0,2:T(8,128)(2,1)S(1)} %copy.11, s32[1024]{0:T(1024)S(1)} %pad_clamp_fusion), kind=kCustom, calls=%fused_computation | custom fusion | bytes 1378304 | tf_op jit(solution)/shard_map/jit(_take)/gather | solution.py:62
  13.6 3.1 %select_bitcast_fusion = bf16[7,96,512]{1,0,2:T(8,128)(2,1)S(1)} fusion(bf16[512,7,96]{2,1,0:T(8,128)(2,1)} %gather_fusion, pred[512]{0:T(512)(128)(4,1)S(1)} %compare_and_fusion), kind=kLoop, calls=%fused_computation.17 | loop fusion | flops 344064 | bytes 1376768 | tf_op jit(solution)/shard_map/jit(_take)/select_n | solution.py:62
  18.6 8.6 %all-gather = f32[192,512]{1,0:T(8,128)S(1)} all-gather(f32[96,512]{1,0:T(8,128)S(1)} %bitcast.40), channel_id=2, replica_groups=mesh['region'=4,'depth'=2,'member'=4] {'depth'}, dimensions={0}, use_global_device_ids=true | all-gather | bytes 589824 | tf_op jit(solution)/shard_map/all_gather | solution.py:64
  27.2 10.7 %all-reduce = (f32[7,1024]{1,0:T(8,128)S(1)}, f32[512]{0:T(512)S(1)}, f32[512]{0:T(512)S(1)}) all-reduce(f32[7,1024]{1,0:T(8,128)S(1)} %convert_reduce_fusion, f32[512]{0:T(512)S(1)} %reduce_sum.55, f32[512]{0:T(512)S(1)} %multiply_reduce_fusion), channel_id=1, replica_groups=mesh['region'=4,'depth'=2,'member'=4] {'member'}, use_global_device_ids=true, to_apply=%region_1.2 | all-reduce | flops 8192 | bytes 65536 | tf_op jit(solution)/shard_map/psum | solution.py:66
  38.6 12.6 %all-reduce.1 = (f32[]{:T(128)}, f32[]{:T(128)}) all-reduce(f32[]{:T(128)} %get-tuple-element.225, f32[]{:T(128)} %get-tuple-element.238), channel_id=1, replica_groups=mesh['region'=4,'depth'=2,'member'=4] {'region'}, use_global_device_ids=true, to_apply=%region_6.7 | all-reduce | flops 2 | bytes 16 | tf_op jit(solution)/shard_map/psum | solution.py:74
  54.0 4.6 %collective-permute-start = (bf16[192,512]{1,0:T(8,128)(2,1)S(1)}, bf16[192,512]{1,0:T(8,128)(2,1)S(1)}, u32[]{:S(2)}, u32[]{:S(2)}) collective-permute-start(bf16[192,512]{1,0:T(8,128)(2,1)S(1)} %pad_maximum_fusion.1), channel_id=1, source_target_pairs={{0,8},{8,16},{16,24},{1,9},{9,17},{17,25},{2,10},{10,18},{18,26},{... | collective-permute-start | bytes 589832 | tf_op jit(solution)/shard_map/ppermute | solution.py:17
  58.5 1.7 %collective-permute-done.1 = bf16[192,512]{1,0:T(8,128)(2,1)S(1)} collective-permute-done((bf16[192,512]{1,0:T(8,128)(2,1)S(1)}, bf16[192,512]{1,0:T(8,128)(2,1)S(1)}, u32[]{:S(2)}, u32[]{:S(2)}) %collective-permute-start.1) | collective-permute-done | bytes 196640 | tf_op jit(solution)/shard_map/ppermute | solution.py:18
  60.2 1.5 collective-permute-done
  62.6 1.4 fusion.18
  65.4 5.0 %collective-permute-start.2 = (f32[2,512]{1,0:T(2,128)S(1)}, f32[2,512]{1,0:T(2,128)S(1)}, u32[]{:S(2)}, u32[]{:S(2)}) collective-permute-start(f32[2,512]{1,0:T(2,128)S(1)} %pad_maximum_fusion.3), channel_id=1, source_target_pairs={{0,8},{8,16},{16,24},{1,9},{9,17},{17,25},{2,10},{10,18},{18,26},{... | collective-permute-start | bytes 12296 | tf_op jit(solution)/shard_map/ppermute | solution.py:17
  70.4 1.3 collective-permute-done.2
  71.7 8.7 %all-gather.6.cloned.1.call-done = bf16[384,1536]{1,0:T(8,128)(2,1)} async-done(((bf16[96,1536]{1,0:T(8,128)(2,1)}), bf16[384,1536]{1,0:T(8,128)(2,1)}) %all-gather.6.cloned.1.call-update) | async-done | bytes 1179664 | tf_op jit(solution)/shard_map/all_gather | solution.py:97
  80.4 44.1 %all-gather.4.cloned.1.call-done = bf16[7,384,1024]{2,1,0:T(8,128)(2,1)} async-done(((bf16[7,96,1024]{2,1,0:T(8,128)(2,1)}), bf16[7,384,1024]{2,1,0:T(8,128)(2,1)}) %all-gather.4.cloned.1.call-update) | async-done | bytes 5505040 | tf_op jit(solution)/shard_map/all_gather | solution.py:96
  124.7 35.0 %while.13 = (s32[]{:T(128)}, bf16[7,96,1024]{2,1,0:T(8,128)(2,1)S(1)}, f32[7,1024]{1,0:T(8,128)S(1)}, f32[]{:T(128)}, bf16[7,96,1024]{2,1,0:T(8,128)(2,1)}, /*in...) while((s32[]{:T(128)}, ...), condition=%wide.region_12.13_spmd, body=%wide.region_11.12_spmd.sunk | while | flops 1325961472 | bytes 4130527 | solution.py:54
  125.0 4.0 %fusion.33 = bf16[7,96,1024]{2,1,0:T(8,128)(2,1)S(1)} fusion(bf16[7,96,1024]{2,1,0:T(8,128)(2,1)S(1)} %get-tuple-element.323, s32[]{:T(128)S(6)} %select_n.27, f32[128,1536]{1,0:T(8,128)S(1)} %multiply_multiply_fusion.2, bf16[384,1536]{1,0:T(8,128)(2,1)} %get-tuple-element.344, bf16[7,384,1024]{2,1,0:T(8,128)(2,1)} %get-tuple-element.343, ...), kind=kOutput, calls=%fused_computation.7.clone.1 | convolution fusion | flops 1324388352 | bytes 3298816 | tf_op jit(solution)/shard_map/while/body/eval_jaxpr/ltj,mj->lmt/dot_general | solution.py:45
  129.4 4.0 %fusion.33 = bf16[7,96,1024]{2,1,0:T(8,128)(2,1)S(1)} fusion(bf16[7,96,1024]{2,1,0:T(8,128)(2,1)S(1)} %get-tuple-element.323, s32[]{:T(128)S(6)} %select_n.27, f32[128,1536]{1,0:T(8,128)S(1)} %multiply_multiply_fusion.2, bf16[384,1536]{1,0:T(8,128)(2,1)} %get-tuple-element.344, bf16[7,384,1024]{2,1,0:T(8,128)(2,1)} %get-tuple-element.343, ...), kind=kOutput, calls=%fused_computation.7.clone.1 | convolution fusion | flops 1324388352 | bytes 3298816 | tf_op jit(solution)/shard_map/while/body/eval_jaxpr/ltj,mj->lmt/dot_general | solution.py:45
  133.8 4.0 %fusion.33 = bf16[7,96,1024]{2,1,0:T(8,128)(2,1)S(1)} fusion(bf16[7,96,1024]{2,1,0:T(8,128)(2,1)S(1)} %get-tuple-element.323, s32[]{:T(128)S(6)} %select_n.27, f32[128,1536]{1,0:T(8,128)S(1)} %multiply_multiply_fusion.2, bf16[384,1536]{1,0:T(8,128)(2,1)} %get-tuple-element.344, bf16[7,384,1024]{2,1,0:T(8,128)(2,1)} %get-tuple-element.343, ...), kind=kOutput, calls=%fused_computation.7.clone.1 | convolution fusion | flops 1324388352 | bytes 3298816 | tf_op jit(solution)/shard_map/while/body/eval_jaxpr/ltj,mj->lmt/dot_general | solution.py:45
  138.2 4.0 %fusion.33 = bf16[7,96,1024]{2,1,0:T(8,128)(2,1)S(1)} fusion(bf16[7,96,1024]{2,1,0:T(8,128)(2,1)S(1)} %get-tuple-element.323, s32[]{:T(128)S(6)} %select_n.27, f32[128,1536]{1,0:T(8,128)S(1)} %multiply_multiply_fusion.2, bf16[384,1536]{1,0:T(8,128)(2,1)} %get-tuple-element.344, bf16[7,384,1024]{2,1,0:T(8,128)(2,1)} %get-tuple-element.343, ...), kind=kOutput, calls=%fused_computation.7.clone.1 | convolution fusion | flops 1324388352 | bytes 3298816 | tf_op jit(solution)/shard_map/while/body/eval_jaxpr/ltj,mj->lmt/dot_general | solution.py:45
  142.5 4.0 %fusion.33 = bf16[7,96,1024]{2,1,0:T(8,128)(2,1)S(1)} fusion(bf16[7,96,1024]{2,1,0:T(8,128)(2,1)S(1)} %get-tuple-element.323, s32[]{:T(128)S(6)} %select_n.27, f32[128,1536]{1,0:T(8,128)S(1)} %multiply_multiply_fusion.2, bf16[384,1536]{1,0:T(8,128)(2,1)} %get-tuple-element.344, bf16[7,384,1024]{2,1,0:T(8,128)(2,1)} %get-tuple-element.343, ...), kind=kOutput, calls=%fused_computation.7.clone.1 | convolution fusion | flops 1324388352 | bytes 3298816 | tf_op jit(solution)/shard_map/while/body/eval_jaxpr/ltj,mj->lmt/dot_general | solution.py:45
  146.9 4.0 %fusion.33 = bf16[7,96,1024]{2,1,0:T(8,128)(2,1)S(1)} fusion(bf16[7,96,1024]{2,1,0:T(8,128)(2,1)S(1)} %get-tuple-element.323, s32[]{:T(128)S(6)} %select_n.27, f32[128,1536]{1,0:T(8,128)S(1)} %multiply_multiply_fusion.2, bf16[384,1536]{1,0:T(8,128)(2,1)} %get-tuple-element.344, bf16[7,384,1024]{2,1,0:T(8,128)(2,1)} %get-tuple-element.343, ...), kind=kOutput, calls=%fused_computation.7.clone.1 | convolution fusion | flops 1324388352 | bytes 3298816 | tf_op jit(solution)/shard_map/while/body/eval_jaxpr/ltj,mj->lmt/dot_general | solution.py:45
  151.3 4.0 %fusion.33 = bf16[7,96,1024]{2,1,0:T(8,128)(2,1)S(1)} fusion(bf16[7,96,1024]{2,1,0:T(8,128)(2,1)S(1)} %get-tuple-element.323, s32[]{:T(128)S(6)} %select_n.27, f32[128,1536]{1,0:T(8,128)S(1)} %multiply_multiply_fusion.2, bf16[384,1536]{1,0:T(8,128)(2,1)} %get-tuple-element.344, bf16[7,384,1024]{2,1,0:T(8,128)(2,1)} %get-tuple-element.343, ...), kind=kOutput, calls=%fused_computation.7.clone.1 | convolution fusion | flops 1324388352 | bytes 3298816 | tf_op jit(solution)/shard_map/while/body/eval_jaxpr/ltj,mj->lmt/dot_general | solution.py:45
  155.6 4.0 %fusion.33 = bf16[7,96,1024]{2,1,0:T(8,128)(2,1)S(1)} fusion(bf16[7,96,1024]{2,1,0:T(8,128)(2,1)S(1)} %get-tuple-element.323, s32[]{:T(128)S(6)} %select_n.27, f32[128,1536]{1,0:T(8,128)S(1)} %multiply_multiply_fusion.2, bf16[384,1536]{1,0:T(8,128)(2,1)} %get-tuple-element.344, bf16[7,384,1024]{2,1,0:T(8,128)(2,1)} %get-tuple-element.343, ...), kind=kOutput, calls=%fused_computation.7.clone.1 | convolution fusion | flops 1324388352 | bytes 3298816 | tf_op jit(solution)/shard_map/while/body/eval_jaxpr/ltj,mj->lmt/dot_general | solution.py:45
  (81 shorter events, 10.1 us)
Async XLA Ops:
  7.2 10.6 %copy-start = (f32[7]{0:T(128)S(1)}, f32[7]{0:T(128)}, u32[]{:S(2)}) copy-start(f32[7]{0:T(128)} %param.9) | copy-start | bytes 88
  7.2 1.8 %copy-start.1 = (bf16[7,96,1024]{2,1,0:T(8,128)(2,1)S(1)}, bf16[7,96,1024]{2,1,0:T(8,128)(2,1)}, u32[]{:S(2)}) copy-start(bf16[7,96,1024]{2,1,0:T(8,128)(2,1)} %param.8) | copy-start | bytes 4128772
  7.2 73.2 %all-gather.6.cloned.1.call-start = ((), (), s32[]{:S(2)}) async-start(), calls=%async_computation.1 | async-start | bytes 1474560 | tf_op jit(solution)/shard_map/all_gather | solution.py:97
  9.0 2.2 %copy-start.4 = (s32[512]{0:T(512)S(1)}, s32[512]{0:T(512)}, u32[]{:S(2)}) copy-start(s32[512]{0:T(512)} %param.10) | copy-start | bytes 6148
  17.7 20.2 %copy-start.5 = (f32[512]{0:T(512)S(1)}, f32[512]{0:T(512)}, u32[]{:S(2)}) copy-start(f32[512]{0:T(512)} %param.12) | copy-start | bytes 6148
  17.8 20.2 %copy-start.6 = (f32[512]{0:T(512)S(1)}, f32[512]{0:T(512)}, u32[]{:S(2)}) copy-start(f32[512]{0:T(512)} %param.11) | copy-start | bytes 6148
  17.8 34.8 %copy-start.3 = (f32[96,512]{1,0:T(8,128)S(1)}, f32[96,512]{1,0:T(8,128)}, u32[]{:S(2)}) copy-start(f32[96,512]{1,0:T(8,128)} %param.13) | copy-start | bytes 589828
  52.7 7.6 %collective-permute-start.1 = (bf16[192,512]{1,0:T(8,128)(2,1)S(1)}, bf16[192,512]{1,0:T(8,128)(2,1)S(1)}, u32[]{:S(2)}, u32[]{:S(2)}) collective-permute-start(bf16[192,512]{1,0:T(8,128)(2,1)S(1)} %pad_maximum_fusion.1), channel_id=1, source_target_pairs={{8,0},{16,8},{24,16},{9,1},{17,9},{25,17},{10,2},{18,10},{26,18},{... | collective-permute-start | bytes 589832 | tf_op jit(solution)/shard_map/ppermute | solution.py:18
  54.0 7.7 %collective-permute-start = (bf16[192,512]{1,0:T(8,128)(2,1)S(1)}, bf16[192,512]{1,0:T(8,128)(2,1)S(1)}, u32[]{:S(2)}, u32[]{:S(2)}) collective-permute-start(bf16[192,512]{1,0:T(8,128)(2,1)S(1)} %pad_maximum_fusion.1), channel_id=1, source_target_pairs={{0,8},{8,16},{16,24},{1,9},{9,17},{17,25},{2,10},{10,18},{18,26},{... | collective-permute-start | bytes 589832 | tf_op jit(solution)/shard_map/ppermute | solution.py:17
  62.5 62.0 %all-gather.4.cloned.1.call-start = ((), (), s32[]{:S(2)}) async-start(), calls=%async_computation | async-start | bytes 6881280 | tf_op jit(solution)/shard_map/all_gather | solution.py:96
  64.1 6.3 %collective-permute-start.3 = (f32[2,512]{1,0:T(2,128)S(1)}, f32[2,512]{1,0:T(2,128)S(1)}, u32[]{:S(2)}, u32[]{:S(2)}) collective-permute-start(f32[2,512]{1,0:T(2,128)S(1)} %pad_maximum_fusion.3), channel_id=1, source_target_pairs={{8,0},{16,8},{24,16},{9,1},{17,9},{25,17},{10,2},{18,10},{26,18},{... | collective-permute-start | bytes 12296 | tf_op jit(solution)/shard_map/ppermute | solution.py:18
  65.4 6.3 %collective-permute-start.2 = (f32[2,512]{1,0:T(2,128)S(1)}, f32[2,512]{1,0:T(2,128)S(1)}, u32[]{:S(2)}, u32[]{:S(2)}) collective-permute-start(f32[2,512]{1,0:T(2,128)S(1)} %pad_maximum_fusion.3), channel_id=1, source_target_pairs={{0,8},{8,16},{16,24},{1,9},{9,17},{17,25},{2,10},{10,18},{18,26},{... | collective-permute-start | bytes 12296 | tf_op jit(solution)/shard_map/ppermute | solution.py:17
  159.6 1.1 copy-start.2
Sparse Core Ops, SparseCore 0:
  62.6 17.7 all-gather.5
  82.6 41.8 all-gather.3
